TPU v7x, 32 devices: a whole 2x2x4 slice. The times are simulated.
32 devices in a mesh: dp: 8 (over z, y), head: 4 (over x, core).
Axes of the slice: x: 2, y: 2, z: 4, core: 2. Of those that a mesh axis runs over, the one named last changes fastest.
Arguments:
- tokens: bfloat16 [32768, 768], P(('dp', 'head')), may hold values from -6 to 6
- seq_lengths: int32 [64, 32], P('dp'), may hold values from 0 to 512, as said below
- qkv_weight: bfloat16 [2, 3, 768, 768], P(None, None, None, 'head'), may hold values from -0.21875 to 0.21875
- qv_bias: float32 [2, 2, 768], P(None, None, 'head'), may hold values from -3 to 3
- out_weight: bfloat16 [2, 768, 768], replicated, may hold values from -0.875 to 0.875
- out_bias: float32 [2, 768], replicated, may hold values from -3 to 3
- norm1_gain: float32 [2, 768], replicated, may hold values from 0.25 to 1.75
- norm1_shift: float32 [2, 768], replicated, may hold values from -3 to 3
- up_weight: bfloat16 [2, 768, 3072], replicated, may hold values from -0.21875 to 0.21875
- up_bias: float32 [2, 3072], replicated, may hold values from -3 to 3
- down_weight: bfloat16 [2, 3072, 768], replicated, may hold values from -0.109375 to 0.109375
- down_bias: float32 [2, 768], replicated, may hold values from -3 to 3
- norm2_gain: float32 [2, 768], replicated, may hold values from 0.25 to 1.75
- norm2_shift: float32 [2, 768], replicated, may hold values from -3 to 3
- out_grad: bfloat16 [32768, 768], P(('dp', 'head')), may hold values from -6 to 6
Outputs:
- out_state: bfloat16 [32768, 768], P(('dp', 'head'))
- input_grad: bfloat16 [32768, 768], P(('dp', 'head'))
- qkv_weight_grad: float32 [2, 3, 768, 768], P(None, None, 'dp', 'head')
- qv_bias_grad: float32 [2, 2, 768], replicated
- out_weight_grad: float32 [2, 768, 768], P(None, 'dp', 'head')
- out_bias_grad: float32 [2, 768], replicated
- norm1_gain_grad: float32 [2, 768], replicated
- norm1_shift_grad: float32 [2, 768], replicated
- up_weight_grad: float32 [2, 768, 3072], P(None, 'dp', 'head')
- up_bias_grad: float32 [2, 3072], replicated
- down_weight_grad: float32 [2, 3072, 768], P(None, 'head', 'dp')
- down_bias_grad: float32 [2, 768], replicated
- norm2_gain_grad: float32 [2, 768], replicated
- norm2_shift_grad: float32 [2, 768], replicated
Inputs may be any that keep to these rules, and one draw needn't show every extreme that they name: `seq_lengths`: each slot's row sums to 512; nonzero entries come first and zero entries mark no sequence; some slot holds a single sequence of 512 rows.
All inputs are finite; a program needn't handle non-finite values.
Results may differ from a plain program's by a relative error of at most 0.025.
Values may be sent and summed in bfloat16 or wider, within the bound.
No kernel may reach another device: no remote copies, remote signals or barrier semaphores. Data moves between devices by JAX's collectives and lax.ppermute only.
A program may use at most 256 MiB of HBM per device.

v0:
```python
import jax
import jax.numpy as jnp
from jax import lax
from jax.sharding import PartitionSpec as P

HD = 64
EPSILON = 1e-06


def norm_rows(values, gain, shift):
    centre = jnp.mean(values, axis=-1, keepdims=True)
    centred = values - centre
    spread = jnp.mean(centred * centred, axis=-1, keepdims=True)
    return centred * lax.rsqrt(spread + EPSILON) * gain + shift


def exact_gelu(values):
    return jax.nn.gelu(values, approximate=False)


def segment_ids(lengths, slot_rows):
    boundary = jnp.cumsum(lengths, axis=1)
    position = jnp.arange(slot_rows, dtype=jnp.int32)
    return jnp.sum((position[None, :, None] >= boundary[:, None, :]).astype(jnp.int32), axis=2)


def slot_scores(queries, keys_in, segments):
    scaling = queries.shape[-1] ** (-0.5)
    scores = (
        jnp.einsum("qhd,khd->hqk", queries, keys_in, preferred_element_type=jnp.float32) * scaling
    )
    inside = (segments[:, None] == segments[None, :])[None]
    return (scores, inside)


def slot_forward(packed):
    queries, keys_in, values_in, segments = packed
    scores, inside = slot_scores(queries, keys_in, segments)
    scores = jnp.where(inside, scores, -1e30)
    peak_score = jnp.max(scores, axis=-1, keepdims=True)
    weights = jnp.exp(scores - peak_score)
    denominator = jnp.sum(weights, axis=-1, keepdims=True)
    probability = (weights / denominator).astype(jnp.bfloat16)
    context = jnp.einsum("hqk,khd->qhd", probability, values_in, preferred_element_type=jnp.float32)
    return (context.astype(jnp.bfloat16), (peak_score + jnp.log(denominator))[..., 0])


def slot_backward(packed):
    queries, keys_in, values_in, grad_context, log_total, segments = packed
    scaling = queries.shape[-1] ** (-0.5)
    scores, inside = slot_scores(queries, keys_in, segments)
    probability = jnp.where(inside, jnp.exp(scores - log_total[..., None]), 0.0)
    grad_prob = jnp.einsum(
        "qhd,khd->hqk", grad_context, values_in, preferred_element_type=jnp.float32
    )
    shares = jnp.sum(probability * grad_prob, axis=-1, keepdims=True)
    grad_score = (probability * (grad_prob - shares)).astype(jnp.bfloat16)
    grad_query = (
        jnp.einsum("hqk,khd->qhd", grad_score, keys_in, preferred_element_type=jnp.float32)
        * scaling
    )
    grad_key = (
        jnp.einsum("hqk,qhd->khd", grad_score, queries, preferred_element_type=jnp.float32)
        * scaling
    )
    grad_value = jnp.einsum(
        "hqk,qhd->khd",
        probability.astype(jnp.bfloat16),
        grad_context,
        preferred_element_type=jnp.float32,
    )
    return (
        grad_query.astype(jnp.bfloat16),
        grad_key.astype(jnp.bfloat16),
        grad_value.astype(jnp.bfloat16),
    )


def on_device(
    tokens,
    seq_lengths,
    qkv_weight,
    qv_bias,
    out_weight,
    out_bias,
    norm1_gain,
    norm1_shift,
    up_weight,
    up_bias,
    down_weight,
    down_bias,
    norm2_gain,
    norm2_shift,
    out_grad,
):
    heads_count = lax.axis_size("head")
    head_index = lax.axis_index("head")
    local_rows, model_width = tokens.shape
    group_rows = local_rows * heads_count
    slots_here = seq_lengths.shape[0]
    slot_rows = group_rows // slots_here
    segments = segment_ids(seq_lengths, slot_rows)
    head_width = qkv_weight.shape[-1]
    local_heads = head_width // HD
    layers = qkv_weight.shape[0]
    qkv_shape = (slots_here, slot_rows, 3, local_heads, HD)
    hidden_state = tokens.astype(jnp.float32)
    kept_values = []
    for layer_index in range(layers):
        gathered = lax.all_gather(hidden_state.astype(jnp.bfloat16), "head", axis=0, tiled=True)
        projected = jnp.einsum(
            "rd,cde->rce", gathered, qkv_weight[layer_index], preferred_element_type=jnp.float32
        )
        bias_rows = jnp.stack(
            [
                qv_bias[layer_index, 0],
                jnp.zeros_like(qv_bias[layer_index, 0]),
                qv_bias[layer_index, 1],
            ]
        )
        projected = (projected + bias_rows[None]).astype(jnp.bfloat16)
        shaped = projected.reshape(qkv_shape)
        context, log_total = lax.map(
            slot_forward, (shaped[:, :, 0], shaped[:, :, 1], shaped[:, :, 2], segments)
        )
        context = context.reshape(group_rows, head_width)
        token_context = lax.all_to_all(context, "head", split_axis=0, concat_axis=1, tiled=True)
        attended = (
            jnp.dot(token_context, out_weight[layer_index], preferred_element_type=jnp.float32)
            + out_bias[layer_index]
        )
        first_sum = hidden_state + attended
        normed = norm_rows(first_sum, norm1_gain[layer_index], norm1_shift[layer_index])
        normed_low = normed.astype(jnp.bfloat16)
        ffn_rows = normed_low
        up_part = up_weight[layer_index]
        up_shift = up_bias[layer_index]
        down_part = down_weight[layer_index]
        before_gelu = jnp.dot(ffn_rows, up_part, preferred_element_type=jnp.float32) + up_shift
        activated = exact_gelu(before_gelu).astype(jnp.bfloat16)
        branch = jnp.dot(activated, down_part, preferred_element_type=jnp.float32)
        second_sum = normed + branch + down_bias[layer_index]
        hidden_state = norm_rows(second_sum, norm2_gain[layer_index], norm2_shift[layer_index])
        kept_values.append(
            (
                gathered,
                projected,
                log_total,
                token_context,
                first_sum,
                ffn_rows,
                up_part,
                down_part,
                before_gelu,
                activated,
                second_sum,
            )
        )
    out_state = hidden_state.astype(jnp.bfloat16)
    grad_state = out_grad.astype(jnp.float32)
    ffn_list, proj_list, attn_list, small_list, shift_list = ([], [], [], [], [])
    for layer_index in reversed(range(layers)):
        (
            gathered,
            projected,
            log_total,
            token_context,
            first_sum,
            ffn_rows,
            up_part,
            down_part,
            before_gelu,
            activated,
            second_sum,
        ) = kept_values[layer_index]
        pull_second = jax.vjp(
            norm_rows, second_sum, norm2_gain[layer_index], norm2_shift[layer_index]
        )[1]
        grad_second, grad_gain2, grad_shift2 = pull_second(grad_state)
        grad_branch = grad_second.astype(jnp.bfloat16)
        grad_down_shift = jnp.sum(grad_branch.astype(jnp.float32), axis=0)
        grad_down = jnp.einsum(
            "rd,rf->df", grad_branch, activated, preferred_element_type=jnp.float32
        )
        grad_act = jnp.einsum(
            "rd,fd->rf", grad_branch, down_part, preferred_element_type=jnp.float32
        )
        pull_gelu = jax.vjp(exact_gelu, before_gelu)[1]
        grad_pre = pull_gelu(grad_act)[0].astype(jnp.bfloat16)
        grad_up_shift = jnp.sum(grad_pre.astype(jnp.float32), axis=0)
        grad_up = jnp.einsum("rd,rf->df", ffn_rows, grad_pre, preferred_element_type=jnp.float32)
        grad_normed_low = jnp.einsum(
            "rf,df->rd", grad_pre, up_part, preferred_element_type=jnp.float32
        )
        grad_normed = grad_second + grad_normed_low
        pull_first = jax.vjp(
            norm_rows, first_sum, norm1_gain[layer_index], norm1_shift[layer_index]
        )[1]
        grad_first, grad_gain1, grad_shift1 = pull_first(grad_normed)
        grad_attended = grad_first.astype(jnp.bfloat16)
        grad_out_shift = jnp.sum(grad_attended.astype(jnp.float32), axis=0)
        grad_out = jnp.einsum(
            "rd,re->de", token_context, grad_attended, preferred_element_type=jnp.float32
        )
        grad_mixed = jnp.einsum(
            "re,de->rd", grad_attended, out_weight[layer_index], preferred_element_type=jnp.float32
        ).astype(jnp.bfloat16)
        grad_context = lax.all_to_all(grad_mixed, "head", split_axis=1, concat_axis=0, tiled=True)
        shaped = projected.reshape(qkv_shape)
        grad_query, grad_key, grad_value = lax.map(
            slot_backward,
            (
                shaped[:, :, 0],
                shaped[:, :, 1],
                shaped[:, :, 2],
                grad_context.reshape(slots_here, slot_rows, local_heads, HD),
                log_total,
                segments,
            ),
        )
        grad_proj = jnp.stack([grad_query, grad_key, grad_value], axis=2).reshape(
            group_rows, 3, head_width
        )
        grad_qkv = jnp.einsum(
            "rd,rce->cde", gathered, grad_proj, preferred_element_type=jnp.float32
        )
        bias_local = jnp.sum(grad_proj.astype(jnp.float32), axis=0)
        qv_local = jnp.stack([bias_local[0], bias_local[2]])
        qv_full = lax.dynamic_update_slice_in_dim(
            jnp.zeros((2, model_width), jnp.float32), qv_local, head_index * head_width, 1
        )
        layer_weights = qkv_weight[layer_index]
        grad_state = grad_first + lax.psum_scatter(
            jnp.einsum(
                "rce,cde->rd", grad_proj, layer_weights, preferred_element_type=jnp.float32
            ).astype(jnp.bfloat16),
            "head",
            scatter_dimension=0,
            tiled=True,
        ).astype(jnp.float32)
        ffn_list.append(jnp.stack([grad_up, grad_down]))
        proj_list.append(grad_out)
        attn_list.append(grad_qkv)
        small_list.append(
            jnp.concatenate(
                [
                    qv_full,
                    jnp.stack(
                        [
                            grad_out_shift,
                            grad_gain1,
                            grad_shift1,
                            grad_down_shift,
                            grad_gain2,
                            grad_shift2,
                        ]
                    ),
                ],
                axis=0,
            )
        )
        shift_list.append(grad_up_shift)
    input_grad = grad_state.astype(jnp.bfloat16)
    ffn_stack = jnp.stack(ffn_list[::-1])
    proj_stack = jnp.stack(proj_list[::-1])
    attn_stack = jnp.stack(attn_list[::-1])
    small_stack = jnp.stack(small_list[::-1])
    shift_stack = jnp.stack(shift_list[::-1])
    ffn_data, proj_data, attn_data = (
        lax.psum_scatter(
            ffn_stack.astype(jnp.bfloat16), "dp", scatter_dimension=2, tiled=True
        ).astype(jnp.float32),
        lax.psum_scatter(
            proj_stack.astype(jnp.bfloat16), "dp", scatter_dimension=1, tiled=True
        ).astype(jnp.float32),
        lax.psum_scatter(
            attn_stack.astype(jnp.bfloat16), "dp", scatter_dimension=2, tiled=True
        ).astype(jnp.float32),
    )
    ffn_head, proj_head = (
        lax.psum_scatter(
            ffn_data.astype(jnp.bfloat16), "head", scatter_dimension=3, tiled=True
        ).astype(jnp.float32),
        lax.psum_scatter(
            proj_data.astype(jnp.bfloat16), "head", scatter_dimension=2, tiled=True
        ).astype(jnp.float32),
    )
    small_sum, shift_sum = lax.psum((small_stack, shift_stack), ("dp", "head"))
    down_weight_grad = jnp.transpose(ffn_head[:, 1], (0, 2, 1))
    return (
        out_state,
        input_grad,
        attn_data,
        small_sum[:, 0:2],
        proj_head,
        small_sum[:, 2],
        small_sum[:, 3],
        small_sum[:, 4],
        ffn_head[:, 0],
        shift_sum,
        down_weight_grad,
        small_sum[:, 5],
        small_sum[:, 6],
        small_sum[:, 7],
    )


def solution(mesh):
    in_specs = (
        P(("dp", "head"), None),
        P("dp", None),
        P(None, None, None, "head"),
        P(None, None, "head"),
        P(),
        P(),
        P(),
        P(),
        P(),
        P(),
        P(),
        P(),
        P(),
        P(),
        P(("dp", "head"), None),
    )
    out_specs = (
        P(("dp", "head"), None),
        P(("dp", "head"), None),
        P(None, None, "dp", "head"),
        P(),
        P(None, "dp", "head"),
        P(),
        P(),
        P(),
        P(None, "dp", "head"),
        P(),
        P(None, "head", "dp"),
        P(),
        P(),
        P(),
    )
    return jax.shard_map(
        on_device, mesh=mesh, in_specs=in_specs, out_specs=out_specs, check_vma=False
    )
```

profile of v0, /device:TPU:0, one launch (start us, length us, event | category | flops | bytes accessed | tf_op | source)
XLA Modules:
  0.0 1406.1 jit_solution(3311266776964060774)
XLA Ops:
  12.9 45.8 %all-gather.3.cloned.1.call-done = bf16[4096,768]{1,0:T(8,128)(2,1)} async-done(((bf16[1024,768]{1,0:T(8,128)(2,1)}), bf16[4096,768]{1,0:T(8,128)(2,1)}) %all-gather.3.cloned.1.call-update) | async-done | bytes 6291472 | tf_op jit(solution)/shard_map/all_gather | solution.py:110
  73.9 35.4 %while.52 = (s32[]{:T(128)}, bf16[8,512,3,64]{1,3,2,0:T(8,128)(2,1)}, f32[8,3,512]{2,1,0:T(4,128)S(1)}, bf16[8,512,3,64]{1,3,2,0:T(8,128)(2,1)}, s32[8,512]{1,0:...) while((s32[]{:T(128)}, ...), condition=%wide.region_5.6_spmd, body=%wide.region_2.5_spmd.sunk | while | flops 211122688 | bytes 11335773 | solution.py:123
  113.8 13.7 all_to_all.52
  139.1 15.2 %all-to-all-done = bf16[4,1024,192]{1,2,0:T(8,128)(2,1)S(1)} async-done(((bf16[4,1024,192]{1,2,0:T(8,128)(2,1)}), bf16[4,1024,192]{1,2,0:T(8,128)(2,1)S(1)}, u32[]{:S(2)}, u32[]{:S(2)}) %all-to-all-start) | async-done | bytes 1572896 | tf_op jit(solution)/shard_map/all_to_all | solution.py:127
  158.9 38.8 %multiply_convert_fusion.3 = (bf16[1024,3072]{1,0:T(8,128)(2,1)}, f32[1024,3072]{1,0:T(8,128)}, f32[1024,3072]{1,0:T(8,128)}) fusion(f32[3072]{0:T(1024)S(1)} %bitcast.494, bf16[2,768,3072]{2,1,0:T(8,128)(2,1)} %param.31, f32[1024,768]{0,1:T(8,128)S(1)} %get-tuple-element.478, f32[768]{0:T(1024)S(1)} %get-tuple-element.347, ...), kind=kOutput, calls=%fused_computation.148 | convolution fusion | flops 5043388416 | bytes 39348224 | tf_op jit(solution)/shard_map/dot_general | solution.py:139
  208.6 46.5 %all-gather.5.cloned.1.call-done = bf16[4096,768]{0,1:T(8,128)(2,1)} async-done(((bf16[1024,768]{0,1:T(8,128)(2,1)}), bf16[4096,768]{0,1:T(8,128)(2,1)}) %all-gather.5.cloned.1.call-update) | async-done | bytes 6291472 | tf_op jit(solution)/shard_map/all_gather | solution.py:110
  273.1 43.5 %while.53 = (s32[]{:T(128)}, bf16[8,512,3,64]{1,3,2,0:T(8,128)(2,1)}, f32[8,3,512]{2,1,0:T(4,128)S(1)}, bf16[8,512,3,64]{1,3,2,0:T(8,128)(2,1)}, s32[8,512]{1,0:...) while((s32[]{:T(128)}, ...), condition=%wide.region_13.14_spmd, body=%wide.region_10.13_spmd.sunk | while | flops 211122688 | bytes 11335773 | solution.py:123
  334.3 17.5 %all-to-all-done.1 = bf16[4,1024,192]{1,2,0:T(8,128)(2,1)} async-done(((bf16[4,1024,192]{1,2,0:T(8,128)(2,1)}), bf16[4,1024,192]{1,2,0:T(8,128)(2,1)}, u32[]{:S(2)}, u32[]{:S(2)}) %all-to-all-start.1) | async-done | bytes 1572896 | tf_op jit(solution)/shard_map/all_to_all | solution.py:127
  356.5 38.4 %multiply_convert_fusion.2 = (bf16[1024,3072]{1,0:T(8,128)(2,1)}, f32[1024,3072]{1,0:T(8,128)}, f32[1024,3072]{1,0:T(8,128)}) fusion(f32[3072]{0:T(1024)S(1)} %bitcast.497, bf16[2,768,3072]{2,1,0:T(8,128)(2,1)} %param.31, f32[1024,768]{0,1:T(8,128)S(1)} %get-tuple-element.483, f32[768]{0:T(1024)S(1)} %copy-done.73, f32[768]{0:T(1024)S(1)} %copy-done.52, ...), kind=kOutput, calls=%fused_computation.135 | convolution fusion | flops 5043388416 | bytes 39348224 | tf_op jit(solution)/shard_map/dot_general | solution.py:139
  411.1 18.2 %convert_reduce_fusion = (f32[3072]{0:T(1024)}, bf16[1024,3072]{1,0:T(8,128)(2,1)}) fusion(f32[1024,3072]{1,0:T(8,128)} %get-tuple-element.435, bf16[1024,768]{0,1:T(8,128)(2,1)S(1)} %get-tuple-element.425, bf16[2,3072,768]{2,1,0:T(8,128)(2,1)} %param.33, f32[1024,3072]{1,0:T(8,128)} %get-tuple-element.484, f32[3072]{0:T(1024)S(1)} %bitcast.498), kind=kOutput, calls=%fused_computation.131 | convolution fusion | flops 4885312512 | bytes 37773312 | tf_op jit(solution)/shard_map/rd,fd->rf/dot_general | solution.py:185
  429.4 11.7 multiply_reduce_fusion.2
  451.5 20.0 %all-to-all-done.2 = bf16[1024,4,192]{0,2,1:T(8,128)(2,1)S(1)} async-done(((bf16[1024,4,192]{0,2,1:T(8,128)(2,1)}), bf16[1024,4,192]{0,2,1:T(8,128)(2,1)S(1)}, u32[]{:S(2)}, u32[]{:S(2)}) %all-to-all-start.2) | async-done | bytes 1572896 | tf_op jit(solution)/shard_map/all_to_all | solution.py:208
  479.6 88.1 %while.54 = (s32[]{:T(128)}, bf16[8,512,3,64]{1,3,2,0:T(8,128)(2,1)S(1)}, bf16[8,512,3,64]{1,3,2,0:T(8,128)(2,1)}, bf16[8,512,3,64]{1,3,2,0:T(8,128)(2,1)}, bf16...) while((s32[]{:T(128)}, ...), condition=%wide.region_24.25_spmd, body=%wide.region_22.24_spmd.sunk | while | flops 511146496 | bytes 26125428 | solution.py:210
  598.8 11.7 fusion.140
  610.5 41.4 %reduce-scatter.12.cloned.1.call-done = bf16[1024,768]{0,1:T(8,128)(2,1)} async-done(((bf16[4096,768]{0,1:T(8,128)(2,1)}), bf16[1024,768]{0,1:T(8,128)(2,1)}) %reduce-scatter.12.cloned.1.call-update) | async-done | bytes 1572880 | tf_op jit(solution)/shard_map/reduce_scatter | solution.py:233
  659.1 18.5 %convert_reduce_fusion.1 = (f32[3072]{0:T(1024)S(1)}, bf16[1024,3072]{1,0:T(8,128)(2,1)}) fusion(f32[1024,3072]{1,0:T(8,128)} %get-tuple-element.437, bf16[1024,768]{0,1:T(8,128)(2,1)} %get-tuple-element.421, bf16[2,3072,768]{2,1,0:T(8,128)(2,1)} %param.33, f32[1024,3072]{1,0:T(8,128)} %get-tuple-element.479, f32[3072]{0:T(1024)S(1)} %bitcast.495), kind=kOutput, calls=%fused_computation.132 | convolution fusion | flops 4885312512 | bytes 37773312 | tf_op jit(solution)/shard_map/rd,fd->rf/dot_general | solution.py:185
  738.1 16.7 %pad_maximum_fusion = bf16[2,2,768,3072]{3,2,1,0:T(8,128)(2,1)} fusion(bf16[1,2,768,3072]{3,2,1,0:T(8,128)(2,1)} %maximum_bitcast_fusion.1, bf16[1,2,768,3072]{3,2,1,0:T(8,128)(2,1)} %maximum_bitcast_fusion), kind=kLoop, calls=%fused_computation.126 | loop fusion | flops 9437184 | bytes 37748736 | tf_op jit(solution)/shard_map/stack | solution.py:264
  802.2 101.9 %while.55 = (s32[]{:T(128)}, bf16[8,512,3,64]{1,3,2,0:T(8,128)(2,1)}, bf16[8,512,3,64]{1,3,2,0:T(8,128)(2,1)}, bf16[8,512,3,64]{1,3,2,0:T(8,128)(2,1)}, bf16[8,5...) while((s32[]{:T(128)}, ...), condition=%wide.region_32.33_spmd, body=%wide.region_30.32_spmd.sunk | while | flops 511146496 | bytes 26125428 | solution.py:210
  966.8 112.1 %reduce-scatter.18.cloned.1.call-done = bf16[2,2,96,3072]{3,2,1,0:T(8,128)(2,1)} async-done(((bf16[2,2,768,3072]{3,2,1,0:T(8,128)(2,1)}), bf16[2,2,96,3072]{3,2,1,0:T(8,128)(2,1)}) %reduce-scatter.18.cloned.1.call-update) | async-done | bytes 2359312 | tf_op jit(solution)/shard_map/reduce_scatter | solution.py:270
  1081.6 122.8 %all-reduce.3.cloned.1.call-done = (f32[2,8,768]{2,0,1:T(2,128)}, f32[2,3072]{1,0:T(2,128)}) async-done(((f32[2,8,768]{2,0,1:T(2,128)}, f32[2,3072]{1,0:T(2,128)}), (f32[2,8,768]{2,0,1:T(2,128)}, f32[2,3072]{1,0:T(2,128)})) %all-reduce.3.cloned.1.call-update) | async-done | bytes 73744 | tf_op jit(solution)/shard_map/psum | solution.py:288
  1207.1 69.8 %reduce-scatter.22.cloned.1.call-done = bf16[96,1152]{1,0:T(8,128)(2,1)} async-done(((bf16[768,1152]{1,0:T(8,128)(2,1)}), bf16[96,1152]{1,0:T(8,128)(2,1)}) %reduce-scatter.22.cloned.1.call-update) | async-done | bytes 221200
  1281.1 18.6 %reduce-scatter.24.cloned.1.call-done = bf16[192,192]{1,0:T(8,128)(2,1)} async-done(((bf16[768,192]{1,0:T(8,128)(2,1)}), bf16[192,192]{1,0:T(8,128)(2,1)}) %reduce-scatter.24.cloned.1.call-update) | async-done | bytes 73744
  1301.4 59.1 %reduce-scatter.14.cloned.1.call-done = bf16[1024,768]{0,1:T(8,128)(2,1)} async-done(((bf16[4096,768]{0,1:T(8,128)(2,1)}), bf16[1024,768]{0,1:T(8,128)(2,1)}) %reduce-scatter.14.cloned.1.call-update) | async-done | bytes 1572880 | tf_op jit(solution)/shard_map/reduce_scatter | solution.py:233
  1366.3 29.9 %reduce-scatter.20.cloned.1.call-done = bf16[2,2,96,768]{3,2,1,0:T(8,128)(2,1)} async-done(((bf16[2,2,96,3072]{3,2,1,0:T(8,128)(2,1)}), bf16[2,2,96,768]{3,2,1,0:T(8,128)(2,1)}) %reduce-scatter.20.cloned.1.call-update) | async-done | bytes 589840 | tf_op jit(solution)/shard_map/reduce_scatter | solution.py:281
  (599 shorter events, 623.1 us)
Async XLA Ops:
  7.2 51.5 %all-gather.3.cloned.1.call-start = ((), (), s32[]{:S(2)}) async-start(), calls=%async_computation.11 | async-start | bytes 7864320 | tf_op jit(solution)/shard_map/all_gather | solution.py:110
  130.6 23.8 %all-to-all-start = ((bf16[4,1024,192]{1,2,0:T(8,128)(2,1)}), bf16[4,1024,192]{1,2,0:T(8,128)(2,1)S(1)}, u32[]{:S(2)}, u32[]{:S(2)}) async-start(bf16[4,1024,192]{1,2,0:T(8,128)(2,1)} %copy.160), calls=%async_computation | async-start | bytes 3145728 | tf_op jit(solution)/shard_map/all_to_all | solution.py:127
  134.3 120.8 %all-gather.5.cloned.1.call-start = ((), (), s32[]{:S(2)}) async-start(), calls=%async_computation.12 | async-start | bytes 7864320 | tf_op jit(solution)/shard_map/all_gather | solution.py:110
  137.9 59.8 %copy-start.50 = (f32[768]{0:T(1024)}, f32[768]{0:T(1024)S(1)}, u32[]{:S(2)}) copy-start(f32[768]{0:T(1024)S(1)} %get-tuple-element.495) | copy-start | bytes 9220
  137.9 59.8 %copy-start.71 = (f32[768]{0:T(1024)}, f32[768]{0:T(1024)S(1)}, u32[]{:S(2)}) copy-start(f32[768]{0:T(1024)S(1)} %get-tuple-element.347) | copy-start | bytes 9220
  138.5 213.3 %copy-start.35 = (f32[768]{0:T(1024)}, f32[768]{0:T(1024)S(1)}, u32[]{:S(2)}) copy-start(f32[768]{0:T(1024)S(1)} %get-tuple-element.497) | copy-start | bytes 9220
  206.4 145.4 %copy-start = (f32[1024,768]{0,1:T(8,128)}, f32[1024,768]{0,1:T(8,128)S(1)}, u32[]{:S(2)}) copy-start(f32[1024,768]{0,1:T(8,128)S(1)} %get-tuple-element.481) | copy-start | bytes 9437188
  206.4 145.4 %copy-start.33 = (f32[1024]{0:T(1024)}, f32[1024]{0:T(1024)S(1)}, u32[]{:S(2)}) copy-start(f32[1024]{0:T(1024)S(1)} %broadcast_multiply_fusion.2) | copy-start | bytes 12292
  206.8 145.0 %copy-start.37 = (f32[1024]{0:T(1024)}, f32[1024]{0:T(1024)S(1)}, u32[]{:S(2)}) copy-start(f32[1024]{0:T(1024)S(1)} %fusion.190) | copy-start | bytes 12292
  327.0 24.8 %all-to-all-start.1 = ((bf16[4,1024,192]{1,2,0:T(8,128)(2,1)}), bf16[4,1024,192]{1,2,0:T(8,128)(2,1)}, u32[]{:S(2)}, u32[]{:S(2)}) async-start(bf16[4,1024,192]{1,2,0:T(8,128)(2,1)} %copy.166), calls=%async_computation.1 | async-start | bytes 3145728 | tf_op jit(solution)/shard_map/all_to_all | solution.py:127
  447.9 23.6 %all-to-all-start.2 = ((bf16[1024,4,192]{0,2,1:T(8,128)(2,1)}), bf16[1024,4,192]{0,2,1:T(8,128)(2,1)S(1)}, u32[]{:S(2)}, u32[]{:S(2)}) async-start(bf16[1024,4,192]{0,2,1:T(8,128)(2,1)} %bitcast.68), calls=%async_computation.2 | async-start | bytes 3145728 | tf_op jit(solution)/shard_map/all_to_all | solution.py:208
  451.4 200.5 %reduce-scatter.12.cloned.1.call-start = ((), (), s32[]{:S(2)}) async-start(), calls=%async_computation.13 | async-start | bytes 7864320 | tf_op jit(solution)/shard_map/reduce_scatter | solution.py:233
  593.4 361.3 %reduce-scatter.16.cloned.1.call-start = ((), (), s32[]{:S(2)}) async-start(), calls=%async_computation.15 | async-start | bytes 2654208 | tf_op jit(solution)/shard_map/reduce_scatter | solution.py:273
  598.8 53.1 %copy-start.1 = (f32[1024,768]{0,1:T(8,128)S(1)}, f32[1024,768]{0,1:T(8,128)}, u32[]{:S(2)}) copy-start(f32[1024,768]{0,1:T(8,128)} %copy-done) | copy-start | bytes 9437188
  598.8 53.1 %copy-start.34 = (f32[1024]{0:T(1024)S(1)}, f32[1024]{0:T(1024)}, u32[]{:S(2)}) copy-start(f32[1024]{0:T(1024)} %copy-done.33) | copy-start | bytes 12292
  598.8 53.1 %copy-start.36 = (f32[768]{0:T(1024)S(1)}, f32[768]{0:T(1024)}, u32[]{:S(2)}) copy-start(f32[768]{0:T(1024)} %copy-done.35) | copy-start | bytes 9220
  598.8 53.1 %copy-start.38 = (f32[1024]{0:T(1024)S(1)}, f32[1024]{0:T(1024)}, u32[]{:S(2)}) copy-start(f32[1024]{0:T(1024)} %copy-done.37) | copy-start | bytes 12292
  693.2 385.8 %reduce-scatter.18.cloned.1.call-start = ((), (), s32[]{:S(2)}) async-start(), calls=%async_computation.16 | async-start | bytes 21233664 | tf_op jit(solution)/shard_map/reduce_scatter | solution.py:270
  763.2 24.5 %all-to-all-start.3 = ((bf16[1024,4,192]{0,2,1:T(8,128)(2,1)}), bf16[1024,4,192]{0,2,1:T(8,128)(2,1)}, u32[]{:S(2)}, u32[]{:S(2)}) async-start(bf16[1024,4,192]{0,2,1:T(8,128)(2,1)} %bitcast.483), calls=%async_computation.4 | async-start | bytes 3145728 | tf_op jit(solution)/shard_map/all_to_all | solution.py:208
  767.6 436.8 %all-reduce.3.cloned.1.call-start = ((), (), s32[]{:S(2)}) async-start(), calls=%async_computation.20 | async-start | bytes 147456 | tf_op jit(solution)/shard_map/psum | solution.py:288
  932.0 344.8 %reduce-scatter.22.cloned.1.call-start = ((), (), s32[]{:S(2)}) async-start(), calls=%async_computation.18 | async-start | bytes 1990656
  954.6 345.0 %reduce-scatter.24.cloned.1.call-start = ((), (), s32[]{:S(2)}) async-start(), calls=%async_computation.19 | async-start | bytes 491520
  957.0 403.6 %reduce-scatter.14.cloned.1.call-start = ((), (), s32[]{:S(2)}) async-start(), calls=%async_computation.14 | async-start | bytes 7864320 | tf_op jit(solution)/shard_map/reduce_scatter | solution.py:233
  966.8 429.4 %reduce-scatter.20.cloned.1.call-start = ((), (), s32[]{:S(2)}) async-start(), calls=%async_computation.17 | async-start | bytes 2949120 | tf_op jit(solution)/shard_map/reduce_scatter | solution.py:281
  (75 other events, 1029.3 us)
Sparse Core Ops, SparseCore 0:
  9.6 49.0 all-gather.2
  208.7 46.3 all-gather.4
  593.5 58.3 reduce-scatter.11
  693.3 69.0 reduce-scatter.15
  766.6 312.3 reduce-scatter.17
  1086.6 117.7 all-reduce.2
  1208.2 68.5 reduce-scatter.21
  1279.9 19.7 reduce-scatter.23
  1302.2 58.3 reduce-scatter.13
  1363.1 33.0 reduce-scatter.19
where the time goes:
time: 1420 us; the launch traced here: 1410 us
  waiting for transfers between devices  610 us (43%)
  matrix products  475 us (33%)
  local copies, waits for them, and re-layouts  185 us (13%)
  other arithmetic  102 us (7%)
  starting transfers between devices  17.2 us (1%)
  between operations  15.7 us (1%)
    psum x1, waiting for transfers between devices, on_device(): small_sum, shift_sum = lax.psum((small_stack, shift_stack), ('dp', 'head'))  123 us
    reduce_scatter x1, waiting for transfers between devices, on_device(): lax.psum_scatter(ffn_stack.astype(jnp.bfloat16), 'dp', scatter_dimension=...  112 us
    reduce_scatter x2, waiting for transfers between devices, on_device(): lax.psum_scatter(jnp.einsum('rce,cde->rd', grad_proj, layer_weights, pref...  101 us
    all_gather x2, waiting for transfers between devices, on_device(): lax.all_gather(hidden_state.astype(jnp.bfloat16), 'head', axis=0, tiled=T...  92.3 us
    unnamed x12, waiting for transfers between devices  89.2 us
    dot_general x2, matrix products, on_device(): jnp.dot(ffn_rows, up_part, preferred_element_type=jnp.float32) + up_shift  77.2 us
    unnamed x195, local copies, waits for them, and re-layouts  57.6 us
    dot_general x32, matrix products, slot_scores(): jnp.einsum('qhd,khd->hqk', queries, keys_in, preferred_element_type=jnp.f...  55.1 us
  transfers between devices with their start and end apart: 14, of which 13 were waited for; matrix products, arithmetic and copies ran while one was open for 21% of the time, Pallas kernels for 0%

commit v1 on v0

--- a/solution.py
+++ b/solution.py
@@ -5,6 +5,18 @@
 
 HD = 64
 EPSILON = 1e-06
+
+
+def doubled_up(x, axis, dim):
+    ways, here = (lax.axis_size(axis), lax.axis_index(axis))
+    grown, reach = (x, 1)
+    while reach < ways:
+        theirs = lax.ppermute(grown, axis, [(d, d ^ reach) for d in range(ways)])
+        mine_first = jnp.concatenate([grown, theirs], axis=dim)
+        theirs_first = jnp.concatenate([theirs, grown], axis=dim)
+        grown = jnp.where(here & reach == 0, mine_first, theirs_first)
+        reach = 2 * reach
+    return grown
 
 
 def norm_rows(values, gain, shift):
@@ -107,7 +119,7 @@
     hidden_state = tokens.astype(jnp.float32)
     kept_values = []
     for layer_index in range(layers):
-        gathered = lax.all_gather(hidden_state.astype(jnp.bfloat16), "head", axis=0, tiled=True)
+        gathered = doubled_up(hidden_state.astype(jnp.bfloat16), "head", 0)
         projected = jnp.einsum(
             "rd,cde->rce", gathered, qkv_weight[layer_index], preferred_element_type=jnp.float32
         )

time: 1420 us -> 1480 us (1.042)
  waiting for transfers between devices: 610 us -> 658 us
    ppermute x0 -> x4, waiting for transfers between devices: none -> 143 us  [doubled_up(): theirs = lax.ppermute(grown, axis, [(d, d ^ reach) for d in range(ways)])]
    all_gather x2 -> x0, waiting for transfers between devices: 92.3 us -> none  [on_device(): lax.all_gather(hidden_state.astype(jnp.bfloat16), 'head', axis=0, tiled=T...]
    unnamed x12 -> x10, waiting for transfers between devices: 89.2 us -> 88.3 us
    unnamed x195 -> x203, local copies, waits for them, and re-layouts: 57.6 us -> 57.9 us
  transfers between devices with their start and end apart: 14 -> 16, of which waited for: 13 -> 15; matrix products, arithmetic and copies ran while one was open for 21% -> 21% of each run, Pallas kernels for 0% -> 0%
where the time goes in v1:
time: 1480 us; the launch traced here: 1460 us
  waiting for transfers between devices  658 us (44%)
  matrix products  485 us (33%)
  local copies, waits for them, and re-layouts  173 us (12%)
  other arithmetic  107 us (7%)
  starting transfers between devices  20.4 us (1%)
  between operations  15.7 us (1%)
    ppermute x4, waiting for transfers between devices, doubled_up(): theirs = lax.ppermute(grown, axis, [(d, d ^ reach) for d in range(ways)])  143 us
    psum x1, waiting for transfers between devices, on_device(): small_sum, shift_sum = lax.psum((small_stack, shift_stack), ('dp', 'head'))  123 us
    reduce_scatter x1, waiting for transfers between devices, on_device(): lax.psum_scatter(ffn_stack.astype(jnp.bfloat16), 'dp', scatter_dimension=...  110 us
    reduce_scatter x2, waiting for transfers between devices, on_device(): lax.psum_scatter(jnp.einsum('rce,cde->rd', grad_proj, layer_weights, pref...  101 us
    unnamed x10, waiting for transfers between devices  88.3 us
    dot_general x2, matrix products, on_device(): jnp.dot(ffn_rows, up_part, preferred_element_type=jnp.float32) + up_shift  77.9 us
    unnamed x203, local copies, waits for them, and re-layouts  57.9 us
    dot_general x32, matrix products, slot_scores(): jnp.einsum('qhd,khd->hqk', queries, keys_in, preferred_element_type=jnp.f...  55.1 us
  transfers between devices with their start and end apart: 16, of which 15 were waited for; matrix products, arithmetic and copies ran while one was open for 21% of the time, Pallas kernels for 0%

profile of v1, /device:TPU:0, one launch (start us, length us, event | category | flops | bytes accessed | tf_op | source)
XLA Modules:
  0.0 1461.1 jit_solution(7953025597665729020)
XLA Ops:
  21.9 66.6 %collective-permute-done.1 = bf16[2048,768]{0,1:T(8,128)(2,1)} collective-permute-done((bf16[2048,768]{0,1:T(8,128)(2,1)}, bf16[2048,768]{0,1:T(8,128)(2,1)}, u32[]{:S(2)}, u32[]{:S(2)}) %collective-permute-start.1) | collective-permute-done | bytes 3145760 | tf_op jit(solution)/shard_map/ppermute | solution.py:14
  106.6 35.6 %while.52 = (s32[]{:T(128)}, bf16[8,512,3,64]{1,3,2,0:T(8,128)(2,1)}, f32[8,3,512]{2,1,0:T(4,128)S(1)}, bf16[8,512,3,64]{1,3,2,0:T(8,128)(2,1)}, s32[8,512]{1,0:...) while((s32[]{:T(128)}, ...), condition=%wide.region_5.6_spmd, body=%wide.region_2.5_spmd.sunk | while | flops 211122688 | bytes 11335773 | solution.py:135
  160.4 16.9 %all-to-all-done = bf16[4,1024,192]{1,2,0:T(8,128)(2,1)S(1)} async-done(((bf16[4,1024,192]{1,2,0:T(8,128)(2,1)}), bf16[4,1024,192]{1,2,0:T(8,128)(2,1)S(1)}, u32[]{:S(2)}, u32[]{:S(2)}) %all-to-all-start) | async-done | bytes 1572896 | tf_op jit(solution)/shard_map/all_to_all | solution.py:139
  181.4 39.3 %multiply_convert_fusion.3 = (bf16[1024,3072]{1,0:T(8,128)(2,1)}, f32[1024,3072]{1,0:T(8,128)}, f32[1024,3072]{1,0:T(8,128)}) fusion(f32[3072]{0:T(1024)S(1)} %bitcast.492, bf16[2,768,3072]{2,1,0:T(8,128)(2,1)} %param.31, f32[1024,768]{0,1:T(8,128)S(1)} %get-tuple-element.478, f32[768]{0:T(1024)S(1)} %get-tuple-element.347, ...), kind=kOutput, calls=%fused_computation.148 | convolution fusion | flops 5043388416 | bytes 39348224 | tf_op jit(solution)/shard_map/dot_general | solution.py:151
  236.5 70.1 %collective-permute-done.3 = bf16[2048,768]{0,1:T(8,128)(2,1)} collective-permute-done((bf16[2048,768]{0,1:T(8,128)(2,1)}, bf16[2048,768]{0,1:T(8,128)(2,1)}, u32[]{:S(2)}, u32[]{:S(2)}) %collective-permute-start.3) | collective-permute-done | bytes 3145760 | tf_op jit(solution)/shard_map/ppermute | solution.py:14
  327.2 43.5 %while.53 = (s32[]{:T(128)}, bf16[8,512,3,64]{1,3,2,0:T(8,128)(2,1)}, f32[8,3,512]{2,1,0:T(4,128)S(1)}, bf16[8,512,3,64]{1,3,2,0:T(8,128)(2,1)}, s32[8,512]{1,0:...) while((s32[]{:T(128)}, ...), condition=%wide.region_13.14_spmd, body=%wide.region_10.13_spmd.sunk | while | flops 211122688 | bytes 11335773 | solution.py:135
  388.4 17.5 %all-to-all-done.1 = bf16[4,1024,192]{1,2,0:T(8,128)(2,1)} async-done(((bf16[4,1024,192]{1,2,0:T(8,128)(2,1)}), bf16[4,1024,192]{1,2,0:T(8,128)(2,1)}, u32[]{:S(2)}, u32[]{:S(2)}) %all-to-all-start.1) | async-done | bytes 1572896 | tf_op jit(solution)/shard_map/all_to_all | solution.py:139
  410.6 38.6 %multiply_convert_fusion.2 = (bf16[1024,3072]{1,0:T(8,128)(2,1)}, f32[1024,3072]{1,0:T(8,128)}, f32[1024,3072]{1,0:T(8,128)}) fusion(f32[3072]{0:T(1024)S(1)} %bitcast.495, bf16[2,768,3072]{2,1,0:T(8,128)(2,1)} %param.31, f32[1024,768]{0,1:T(8,128)S(1)} %get-tuple-element.483, f32[768]{0:T(1024)S(1)} %copy-done.75, f32[768]{0:T(1024)S(1)} %copy-done.54, ...), kind=kOutput, calls=%fused_computation.135 | convolution fusion | flops 5043388416 | bytes 39348224 | tf_op jit(solution)/shard_map/dot_general | solution.py:151
  465.5 18.1 %convert_reduce_fusion = (f32[3072]{0:T(1024)}, bf16[1024,3072]{1,0:T(8,128)(2,1)}) fusion(f32[1024,3072]{1,0:T(8,128)} %get-tuple-element.435, bf16[1024,768]{0,1:T(8,128)(2,1)S(1)} %get-tuple-element.425, bf16[2,3072,768]{2,1,0:T(8,128)(2,1)} %param.33, f32[1024,3072]{1,0:T(8,128)} %get-tuple-element.484, f32[3072]{0:T(1024)S(1)} %bitcast.496), kind=kOutput, calls=%fused_computation.131 | convolution fusion | flops 4885312512 | bytes 37773312 | tf_op jit(solution)/shard_map/rd,fd->rf/dot_general | solution.py:197
  483.6 11.7 multiply_reduce_fusion.2
  505.7 20.0 %all-to-all-done.2 = bf16[1024,4,192]{0,2,1:T(8,128)(2,1)S(1)} async-done(((bf16[1024,4,192]{0,2,1:T(8,128)(2,1)}), bf16[1024,4,192]{0,2,1:T(8,128)(2,1)S(1)}, u32[]{:S(2)}, u32[]{:S(2)}) %all-to-all-start.2) | async-done | bytes 1572896 | tf_op jit(solution)/shard_map/all_to_all | solution.py:220
  533.8 88.1 %while.54 = (s32[]{:T(128)}, bf16[8,512,3,64]{1,3,2,0:T(8,128)(2,1)S(1)}, bf16[8,512,3,64]{1,3,2,0:T(8,128)(2,1)}, bf16[8,512,3,64]{1,3,2,0:T(8,128)(2,1)}, bf16...) while((s32[]{:T(128)}, ...), condition=%wide.region_24.25_spmd, body=%wide.region_22.24_spmd.sunk | while | flops 511146496 | bytes 26125428 | solution.py:222
  653.1 12.0 fusion.140
  665.1 41.6 %reduce-scatter.12.cloned.1.call-done = bf16[1024,768]{0,1:T(8,128)(2,1)} async-done(((bf16[4096,768]{0,1:T(8,128)(2,1)}), bf16[1024,768]{0,1:T(8,128)(2,1)}) %reduce-scatter.12.cloned.1.call-update) | async-done | bytes 1572880 | tf_op jit(solution)/shard_map/reduce_scatter | solution.py:245
  714.1 18.5 %convert_reduce_fusion.1 = (f32[3072]{0:T(1024)S(1)}, bf16[1024,3072]{1,0:T(8,128)(2,1)}) fusion(f32[1024,3072]{1,0:T(8,128)} %get-tuple-element.437, bf16[1024,768]{0,1:T(8,128)(2,1)} %get-tuple-element.421, bf16[2,3072,768]{2,1,0:T(8,128)(2,1)} %param.33, f32[1024,3072]{1,0:T(8,128)} %get-tuple-element.479, f32[3072]{0:T(1024)S(1)} %bitcast.493), kind=kOutput, calls=%fused_computation.132 | convolution fusion | flops 4885312512 | bytes 37773312 | tf_op jit(solution)/shard_map/rd,fd->rf/dot_general | solution.py:197
  793.0 16.7 %pad_maximum_fusion = bf16[2,2,768,3072]{3,2,1,0:T(8,128)(2,1)} fusion(bf16[1,2,768,3072]{3,2,1,0:T(8,128)(2,1)} %maximum_bitcast_fusion.1, bf16[1,2,768,3072]{3,2,1,0:T(8,128)(2,1)} %maximum_bitcast_fusion), kind=kLoop, calls=%fused_computation.126 | loop fusion | flops 9437184 | bytes 37748736 | tf_op jit(solution)/shard_map/stack | solution.py:276
  822.6 11.2 fusion.173
  857.2 101.9 %while.55 = (s32[]{:T(128)}, bf16[8,512,3,64]{1,3,2,0:T(8,128)(2,1)}, bf16[8,512,3,64]{1,3,2,0:T(8,128)(2,1)}, bf16[8,512,3,64]{1,3,2,0:T(8,128)(2,1)}, bf16[8,5...) while((s32[]{:T(128)}, ...), condition=%wide.region_32.33_spmd, body=%wide.region_30.32_spmd.sunk | while | flops 511146496 | bytes 26125428 | solution.py:222
  1023.9 110.1 %reduce-scatter.18.cloned.1.call-done = bf16[2,2,96,3072]{3,2,1,0:T(8,128)(2,1)} async-done(((bf16[2,2,768,3072]{3,2,1,0:T(8,128)(2,1)}), bf16[2,2,96,3072]{3,2,1,0:T(8,128)(2,1)}) %reduce-scatter.18.cloned.1.call-update) | async-done | bytes 2359312 | tf_op jit(solution)/shard_map/reduce_scatter | solution.py:282
  1136.6 122.8 %all-reduce.3.cloned.1.call-done = (f32[2,8,768]{2,0,1:T(2,128)}, f32[2,3072]{1,0:T(2,128)}) async-done(((f32[2,8,768]{2,0,1:T(2,128)}, f32[2,3072]{1,0:T(2,128)}), (f32[2,8,768]{2,0,1:T(2,128)}, f32[2,3072]{1,0:T(2,128)})) %all-reduce.3.cloned.1.call-update) | async-done | bytes 73744 | tf_op jit(solution)/shard_map/psum | solution.py:300
  1262.1 69.7 %reduce-scatter.22.cloned.1.call-done = bf16[96,1152]{1,0:T(8,128)(2,1)} async-done(((bf16[768,1152]{1,0:T(8,128)(2,1)}), bf16[96,1152]{1,0:T(8,128)(2,1)}) %reduce-scatter.22.cloned.1.call-update) | async-done | bytes 221200
  1336.1 18.4 %reduce-scatter.24.cloned.1.call-done = bf16[192,192]{1,0:T(8,128)(2,1)} async-done(((bf16[768,192]{1,0:T(8,128)(2,1)}), bf16[192,192]{1,0:T(8,128)(2,1)}) %reduce-scatter.24.cloned.1.call-update) | async-done | bytes 73744
  1356.3 59.1 %reduce-scatter.14.cloned.1.call-done = bf16[1024,768]{0,1:T(8,128)(2,1)} async-done(((bf16[4096,768]{0,1:T(8,128)(2,1)}), bf16[1024,768]{0,1:T(8,128)(2,1)}) %reduce-scatter.14.cloned.1.call-update) | async-done | bytes 1572880 | tf_op jit(solution)/shard_map/reduce_scatter | solution.py:245
  1421.2 30.1 %reduce-scatter.20.cloned.1.call-done = bf16[2,2,96,768]{3,2,1,0:T(8,128)(2,1)} async-done(((bf16[2,2,96,3072]{3,2,1,0:T(8,128)(2,1)}), bf16[2,2,96,768]{3,2,1,0:T(8,128)(2,1)}) %reduce-scatter.20.cloned.1.call-update) | async-done | bytes 589840 | tf_op jit(solution)/shard_map/reduce_scatter | solution.py:293
  (611 shorter events, 635.2 us)
Async XLA Ops:
  8.9 3.7 collective-permute-start
  16.9 71.6 %collective-permute-start.1 = (bf16[2048,768]{0,1:T(8,128)(2,1)}, bf16[2048,768]{0,1:T(8,128)(2,1)}, u32[]{:S(2)}, u32[]{:S(2)}) collective-permute-start(bf16[2048,768]{0,1:T(8,128)(2,1)} %maximum_select_fusion.2), channel_id=1, source_target_pairs={{0,2},{1,3},{2,0},{3,1},{4,6},{5,7},{6,4},{7,5},{8,10},{9,11},{10,... | collective-permute-start | bytes 9437192 | tf_op jit(solution)/shard_map/ppermute | solution.py:14
  153.6 23.7 %all-to-all-start = ((bf16[4,1024,192]{1,2,0:T(8,128)(2,1)}), bf16[4,1024,192]{1,2,0:T(8,128)(2,1)S(1)}, u32[]{:S(2)}, u32[]{:S(2)}) async-start(bf16[4,1024,192]{1,2,0:T(8,128)(2,1)} %copy.179), calls=%async_computation | async-start | bytes 3145728 | tf_op jit(solution)/shard_map/all_to_all | solution.py:139
  159.2 61.5 %copy-start.52 = (f32[768]{0:T(1024)}, f32[768]{0:T(1024)S(1)}, u32[]{:S(2)}) copy-start(f32[768]{0:T(1024)S(1)} %get-tuple-element.495) | copy-start | bytes 9220
  159.2 61.6 %copy-start.73 = (f32[768]{0:T(1024)}, f32[768]{0:T(1024)S(1)}, u32[]{:S(2)}) copy-start(f32[768]{0:T(1024)S(1)} %get-tuple-element.347) | copy-start | bytes 9220
  159.8 246.1 %copy-start.37 = (f32[768]{0:T(1024)}, f32[768]{0:T(1024)S(1)}, u32[]{:S(2)}) copy-start(f32[768]{0:T(1024)S(1)} %get-tuple-element.497) | copy-start | bytes 9220
  229.4 176.5 %copy-start = (f32[1024,768]{0,1:T(8,128)}, f32[1024,768]{0,1:T(8,128)S(1)}, u32[]{:S(2)}) copy-start(f32[1024,768]{0,1:T(8,128)S(1)} %get-tuple-element.481) | copy-start | bytes 9437188
  229.4 176.5 %copy-start.35 = (f32[1024]{0:T(1024)}, f32[1024]{0:T(1024)S(1)}, u32[]{:S(2)}) copy-start(f32[1024]{0:T(1024)S(1)} %broadcast_multiply_fusion.2) | copy-start | bytes 12292
  229.9 176.1 %copy-start.39 = (f32[1024]{0:T(1024)}, f32[1024]{0:T(1024)S(1)}, u32[]{:S(2)}) copy-start(f32[1024]{0:T(1024)S(1)} %fusion.192) | copy-start | bytes 12292
  230.4 3.5 collective-permute-start.2
  236.2 70.5 %collective-permute-start.3 = (bf16[2048,768]{0,1:T(8,128)(2,1)}, bf16[2048,768]{0,1:T(8,128)(2,1)}, u32[]{:S(2)}, u32[]{:S(2)}) collective-permute-start(bf16[2048,768]{0,1:T(8,128)(2,1)} %maximum_select_fusion.3), channel_id=1, source_target_pairs={{0,2},{1,3},{2,0},{3,1},{4,6},{5,7},{6,4},{7,5},{8,10},{9,11},{10,... | collective-permute-start | bytes 9437192 | tf_op jit(solution)/shard_map/ppermute | solution.py:14
  381.1 24.8 %all-to-all-start.1 = ((bf16[4,1024,192]{1,2,0:T(8,128)(2,1)}), bf16[4,1024,192]{1,2,0:T(8,128)(2,1)}, u32[]{:S(2)}, u32[]{:S(2)}) async-start(bf16[4,1024,192]{1,2,0:T(8,128)(2,1)} %copy.185), calls=%async_computation.1 | async-start | bytes 3145728 | tf_op jit(solution)/shard_map/all_to_all | solution.py:139
  502.1 23.6 %all-to-all-start.2 = ((bf16[1024,4,192]{0,2,1:T(8,128)(2,1)}), bf16[1024,4,192]{0,2,1:T(8,128)(2,1)S(1)}, u32[]{:S(2)}, u32[]{:S(2)}) async-start(bf16[1024,4,192]{0,2,1:T(8,128)(2,1)} %bitcast.68), calls=%async_computation.2 | async-start | bytes 3145728 | tf_op jit(solution)/shard_map/all_to_all | solution.py:220
  505.7 201.1 %reduce-scatter.12.cloned.1.call-start = ((), (), s32[]{:S(2)}) async-start(), calls=%async_computation.11 | async-start | bytes 7864320 | tf_op jit(solution)/shard_map/reduce_scatter | solution.py:245
  647.7 364.3 %reduce-scatter.16.cloned.1.call-start = ((), (), s32[]{:S(2)}) async-start(), calls=%async_computation.13 | async-start | bytes 2654208 | tf_op jit(solution)/shard_map/reduce_scatter | solution.py:285
  653.1 53.6 %copy-start.36 = (f32[1024]{0:T(1024)S(1)}, f32[1024]{0:T(1024)}, u32[]{:S(2)}) copy-start(f32[1024]{0:T(1024)} %copy-done.35) | copy-start | bytes 12292
  653.1 53.6 %copy-start.38 = (f32[768]{0:T(1024)S(1)}, f32[768]{0:T(1024)}, u32[]{:S(2)}) copy-start(f32[768]{0:T(1024)} %copy-done.37) | copy-start | bytes 9220
  748.2 385.9 %reduce-scatter.18.cloned.1.call-start = ((), (), s32[]{:S(2)}) async-start(), calls=%async_computation.14 | async-start | bytes 21233664 | tf_op jit(solution)/shard_map/reduce_scatter | solution.py:282
  818.2 24.5 %all-to-all-start.3 = ((bf16[1024,4,192]{0,2,1:T(8,128)(2,1)}), bf16[1024,4,192]{0,2,1:T(8,128)(2,1)}, u32[]{:S(2)}, u32[]{:S(2)}) async-start(bf16[1024,4,192]{0,2,1:T(8,128)(2,1)} %bitcast.481), calls=%async_computation.4 | async-start | bytes 3145728 | tf_op jit(solution)/shard_map/all_to_all | solution.py:220
  822.6 436.9 %all-reduce.3.cloned.1.call-start = ((), (), s32[]{:S(2)}) async-start(), calls=%async_computation.18 | async-start | bytes 147456 | tf_op jit(solution)/shard_map/psum | solution.py:300
  987.2 344.7 %reduce-scatter.22.cloned.1.call-start = ((), (), s32[]{:S(2)}) async-start(), calls=%async_computation.16 | async-start | bytes 1990656
  1011.9 342.6 %reduce-scatter.24.cloned.1.call-start = ((), (), s32[]{:S(2)}) async-start(), calls=%async_computation.17 | async-start | bytes 491520
  1014.3 401.2 %reduce-scatter.14.cloned.1.call-start = ((), (), s32[]{:S(2)}) async-start(), calls=%async_computation.12 | async-start | bytes 7864320 | tf_op jit(solution)/shard_map/reduce_scatter | solution.py:245
  1023.9 427.4 %reduce-scatter.20.cloned.1.call-start = ((), (), s32[]{:S(2)}) async-start(), calls=%async_computation.15 | async-start | bytes 2949120 | tf_op jit(solution)/shard_map/reduce_scatter | solution.py:293
  (81 other events, 1193.7 us)
Sparse Core Ops, SparseCore 0:
  647.8 58.9 reduce-scatter.11
  748.3 68.9 reduce-scatter.15
  821.7 312.3 reduce-scatter.17
  1141.6 117.7 all-reduce.2
  1263.1 68.6 reduce-scatter.21
  1334.8 19.7 reduce-scatter.23
  1357.1 58.3 reduce-scatter.13
  1418.2 33.0 reduce-scatter.19
